TPU v7x, 32 devices: a whole 2x2x4 slice. The times are simulated.
32 devices in a mesh: groups: 2 (over x), seq: 16 (over z, y, core).
Axes of the slice: x: 2, y: 2, z: 4, core: 2. Of those that a mesh axis runs over, the one named last changes fastest.
Arguments:
- query_block: bfloat16 [512, 4096], P(('groups', 'seq')), parts along dimension 0, may hold values from -112 to 112
- cache_keys: bfloat16 [8192, 2048], P(('groups', 'seq')), parts along dimension 0, may hold values from -4 to 4
- stored_values: bfloat16 [8192, 2048], P(('groups', 'seq')), parts along dimension 0, may hold values from -6 to 6
- live_counts: int32 [32], P(('groups', 'seq')), parts along dimension 0, may hold values from 128 to 256
- first_position: int32 [2], P('groups'), parts along dimension 0, may hold values from 0 to 3840
- out_weight: bfloat16 [4096, 5376], P('seq'), may hold values from -0.09375 to 0.09375
Outputs:
- attended: bfloat16 [512, 5376], P(('groups', 'seq')), parts along dimension 0
There are 2 independent parts, one for each index of `groups`. A program takes and returns all parts, laid end to end along the dimension named above; an argument that names none is the same for every part. Nothing has to cross between parts.
Inputs may be any that keep to these rules, and one draw needn't show every extreme that they name: `live_counts`: the live slots of a block are its first ones.
All inputs are finite; a program needn't handle non-finite values.
Results may differ from a plain program's by a relative error of at most 0.0058.
Values may be sent and summed in bfloat16 or wider, within the bound.
No kernel may reach another device: no remote copies, remote signals or barrier semaphores. Data moves between devices by JAX's collectives and lax.ppermute only.
A program may use at most 64 MiB of HBM per device.

v0:
```python
import jax
import jax.numpy as jnp
from jax import lax
from jax.sharding import PartitionSpec as P

QUERY_HEADS = 32
KEY_VALUE_HEADS = 16
HEAD_SIZE = 128
score_scale = 168.0 ** (-0.5)
masked_value = -1e30


def head_partial(query_cols, key_cols, value_cols, allowed, group_width):
    row_count = query_cols.shape[0]
    grouped = query_cols.reshape(row_count, group_width, HEAD_SIZE)
    scores = (
        jnp.einsum("rgd,kd->grk", grouped, key_cols, preferred_element_type=jnp.float32)
        * score_scale
    )
    row_best = jnp.max(jnp.where(allowed[None], scores, masked_value), axis=2)
    shifted = jnp.where(allowed[None], scores - row_best[:, :, None], -jnp.inf)
    weights = jnp.exp(shifted)
    weight_sum = jnp.sum(weights, axis=2)
    safe_total = jnp.where(weight_sum > 0, weight_sum, 1.0)
    weighted = jnp.einsum(
        "grk,kd->grd", weights.astype(jnp.bfloat16), value_cols, preferred_element_type=jnp.float32
    )
    value_partial_sum = (weighted / safe_total[:, :, None]).astype(jnp.bfloat16)
    log_sum_exp = jnp.where(weight_sum > 0, row_best + jnp.log(safe_total), masked_value)
    return (value_partial_sum, log_sum_exp)


def merge_sources(received, totals):
    largest = jnp.max(totals, axis=0)
    scales = jnp.exp(totals - largest[None])
    blended = jnp.sum(scales[..., None] * received.astype(jnp.float32), axis=0)
    return (blended / jnp.sum(scales, axis=0)[..., None]).astype(jnp.bfloat16)


def body(query_block, cache_keys, stored_values, live_counts, first_position, out_weight):
    devices = lax.axis_size("seq")
    source = lax.axis_index("seq")
    key_count = cache_keys.shape[0]
    row_total = query_block.shape[0] * devices
    per_group = QUERY_HEADS // devices
    group_width = QUERY_HEADS // KEY_VALUE_HEADS
    first_key = source * key_count
    live_count = live_counts[0]
    begin_pos = first_position[0]
    key_index = lax.iota(jnp.int32, key_count)
    piece_rows = lax.all_gather(query_block, "seq", axis=0, tiled=True)
    row_count = piece_rows.shape[0]
    query_pos = begin_pos + lax.iota(jnp.int32, row_count)
    allowed = (key_index[None, :] < live_count) & (
        first_key + key_index[None, :] <= query_pos[:, None]
    )

    def single_head(key_value_head):
        query_cols = lax.dynamic_slice_in_dim(
            piece_rows, key_value_head * (group_width * HEAD_SIZE), group_width * HEAD_SIZE, 1
        )
        key_cols = lax.dynamic_slice_in_dim(cache_keys, key_value_head * HEAD_SIZE, HEAD_SIZE, 1)
        value_cols = lax.dynamic_slice_in_dim(
            stored_values, key_value_head * HEAD_SIZE, HEAD_SIZE, 1
        )
        return head_partial(query_cols, key_cols, value_cols, allowed, group_width)

    value_partial_sum, log_sum_exp = lax.map(
        single_head, jnp.arange(KEY_VALUE_HEADS, dtype=jnp.int32)
    )
    value_partial_sum = jnp.transpose(value_partial_sum, (2, 0, 1, 3)).reshape(
        row_count, QUERY_HEADS, HEAD_SIZE
    )
    log_sum_exp = jnp.transpose(log_sum_exp, (2, 0, 1)).reshape(row_count, QUERY_HEADS)
    value_partial_sum, log_sum_exp = (value_partial_sum, log_sum_exp)
    value_partial_sum, log_sum_exp = (value_partial_sum, log_sum_exp)
    received = lax.all_to_all(
        value_partial_sum[None], "seq", split_axis=2, concat_axis=0, tiled=True
    )
    totals = lax.all_to_all(log_sum_exp[None], "seq", split_axis=2, concat_axis=0, tiled=True)
    merged = merge_sources(received, totals)
    flattened = merged.reshape(row_total, per_group * HEAD_SIZE)
    summed = lax.psum_scatter(
        jnp.dot(flattened, out_weight, preferred_element_type=jnp.float32),
        "seq",
        scatter_dimension=0,
        tiled=True,
    )
    return summed.astype(jnp.bfloat16)


def solution(mesh):
    in_specs = (
        P(("groups", "seq"), None),
        P(("groups", "seq"), None),
        P(("groups", "seq"), None),
        P(("groups", "seq")),
        P("groups"),
        P("seq", None),
    )
    out_specs = P(("groups", "seq"), None)
    return jax.shard_map(body, mesh=mesh, in_specs=in_specs, out_specs=out_specs, check_vma=False)
```

profile of v0, /device:TPU:0, one launch (start us, length us, event | category | flops | bytes accessed | tf_op | source)
XLA Modules:
  0.0 307.4 jit_solution(6038253713847439832)
XLA Ops:
  8.7 45.0 %all-gather.2.cloned.1.call-done = bf16[256,4096]{1,0:T(8,128)(2,1)} async-done(((bf16[16,4096]{1,0:T(8,128)(2,1)}), bf16[256,4096]{1,0:T(8,128)(2,1)}) %all-gather.2.cloned.1.call-update) | async-done | bytes 2097168 | tf_op jit(solution)/shard_map/all_gather | solution.py:51
  53.7 97.2 %while.13 = (s32[]{:T(128)}, bf16[16,2,256,128]{3,2,1,0:T(8,128)(2,1)}, f32[16,2,256]{2,1,0:T(2,128)S(1)}, s32[16]{0:T(128)S(1)}, bf16[256,2048]{1,0:T(8,128)(2,...) while((s32[]{:T(128)}, ...), condition=%wide.region_3.4_spmd.clone, body=%wide.region_0.3_spmd.clone.sunk | while | flops 68552712 | bytes 2775577 | solution.py:68
  58.0 1.8 fusion.40
  64.0 1.8 fusion.40
  70.1 1.8 fusion.40
  76.2 1.8 fusion.40
  82.3 1.8 fusion.40
  88.3 1.8 fusion.40
  94.4 1.8 fusion.40
  100.5 1.8 fusion.40
  106.6 1.8 fusion.40
  112.6 1.8 fusion.40
  118.7 1.8 fusion.40
  124.8 1.8 fusion.40
  130.9 1.8 fusion.40
  136.9 1.8 fusion.40
  143.0 1.8 fusion.40
  149.1 1.8 fusion.40
  151.0 9.9 %all_to_all.27 = f32[1,256,32]{1,0,2:T(1,128)S(1)} all-to-all(f32[1,256,32]{1,0,2:T(1,128)S(1)} %broadcast_in_dim_reshape.6), channel_id=1, replica_groups=mesh['groups'=2,'seq'=16] {'seq'}, dimensions={2} | all-to-all | bytes 65536 | tf_op jit(solution)/shard_map/all_to_all | solution.py:80
  160.8 4.4 %all-to-all-start.1 = ((bf16[1,256,32,128]{3,1,0,2:T(8,128)(2,1)}), bf16[1,256,32,128]{3,1,0,2:T(8,128)(2,1)}, u32[]{:S(2)}, u32[]{:S(2)}) async-start(bf16[1,256,32,128]{3,1,0,2:T(8,128)(2,1)} %bitcast.71), calls=%async_computation.1 | async-start | bytes 4194304 | tf_op jit(solution)/shard_map/all_to_all | solution.py:77
  165.4 40.8 %all-to-all-done.1 = bf16[1,256,32,128]{3,1,0,2:T(8,128)(2,1)} async-done(((bf16[1,256,32,128]{3,1,0,2:T(8,128)(2,1)}), bf16[1,256,32,128]{3,1,0,2:T(8,128)(2,1)}, u32[]{:S(2)}, u32[]{:S(2)}) %all-to-all-start.1) | async-done | bytes 2097184 | tf_op jit(solution)/shard_map/all_to_all | solution.py:77
  206.2 2.5 fusion.22
  209.0 3.3 %fusion.26 = f32[256,5376]{1,0:T(8,128)} fusion(bf16[256,256]{0,1:T(8,128)(2,1)S(1)} %bitcast.72, bf16[256,5376]{1,0:T(8,128)(2,1)S(1)} %copy-done), kind=kOutput, calls=%fused_computation.39 | convolution fusion | flops 704643072 | bytes 8388608 | tf_op jit(solution)/shard_map/dot_general | solution.py:84
  212.4 86.6 %reduce-scatter.2.cloned.1.call-done = f32[16,5376]{1,0:T(8,128)} async-done(((f32[256,5376]{1,0:T(8,128)}), f32[16,5376]{1,0:T(8,128)}) %reduce-scatter.2.cloned.1.call-update) | async-done | bytes 344080 | tf_op jit(solution)/shard_map/reduce_scatter | solution.py:83
  (145 shorter events, 50.3 us)
Async XLA Ops:
  6.5 202.5 %copy-start = (bf16[256,5376]{1,0:T(8,128)(2,1)S(1)}, bf16[256,5376]{1,0:T(8,128)(2,1)}, u32[]{:S(2)}) copy-start(bf16[256,5376]{1,0:T(8,128)(2,1)} %param.13) | copy-start | bytes 8257540
  6.5 47.2 %all-gather.2.cloned.1.call-start = ((), (), s32[]{:S(2)}) async-start(), calls=%async_computation.3 | async-start | bytes 2228224 | tf_op jit(solution)/shard_map/all_gather | solution.py:51
  160.8 45.4 %all-to-all-start.1 = ((bf16[1,256,32,128]{3,1,0,2:T(8,128)(2,1)}), bf16[1,256,32,128]{3,1,0,2:T(8,128)(2,1)}, u32[]{:S(2)}, u32[]{:S(2)}) async-start(bf16[1,256,32,128]{3,1,0,2:T(8,128)(2,1)} %bitcast.71), calls=%async_computation.1 | async-start | bytes 4194304 | tf_op jit(solution)/shard_map/all_to_all | solution.py:77
  165.3 133.6 %reduce-scatter.2.cloned.1.call-start = ((), (), s32[]{:S(2)}) async-start(), calls=%async_computation.4 | async-start | bytes 5849088 | tf_op jit(solution)/shard_map/reduce_scatter | solution.py:83
Sparse Core Ops, SparseCore 0:
  9.5 44.1 all-gather.1
  212.5 86.3 reduce-scatter.1
where the time goes:
time: 310 us; the launch traced here: 307 us
  waiting for transfers between devices  173 us (56%)
  matrix products  49.7 us (16%)
  local copies, waits for them, and re-layouts  25.9 us (8%)
  loops' own time  20.5 us (7%)
  between operations  14.9 us (5%)
  blocking collectives  9.87 us (3%)
  other arithmetic  9 us (3%)
  starting transfers between devices  4.47 us (1%)
    reduce_scatter x1, waiting for transfers between devices, body(): lax.psum_scatter(jnp.dot(flattened, out_weight, preferred_element_type=jn...  86.6 us
    all_gather x1, waiting for transfers between devices, body(): piece_rows = lax.all_gather(query_block, 'seq', axis=0, tiled=True)  45 us
    all_to_all x1, waiting for transfers between devices, body(): lax.all_to_all(value_partial_sum[None], 'seq', split_axis=2, concat_axis=...  40.8 us
    dot_general x16, matrix products, head_partial(): jnp.einsum('grk,kd->grd', weights.astype(jnp.bfloat16), value_cols, prefe...  29.2 us
    another operation x1, loops' own time, body(): lax.map(single_head, jnp.arange(KEY_VALUE_HEADS, dtype=jnp.int32))  20.5 us
    dot_general x16, matrix products, head_partial(): jnp.einsum('rgd,kd->grk', grouped, key_cols, preferred_element_type=jnp.f...  17.1 us
    dynamic_slice x32, local copies, waits for them, and re-layouts, single_head(): lax.dynamic_slice_in_dim(piece_rows, key_value_head * (group_width * HEAD...  16.3 us
    all_to_all x1, blocking collectives, body(): lax.all_to_all(log_sum_exp[None], 'seq', split_axis=2, concat_axis=0, til...  9.87 us
  transfers between devices with their start and end apart: 3, of which 3 were waited for; matrix products, arithmetic and copies ran while one was open for 0% of the time, Pallas kernels for 0%

commit v1 on v0

--- a/solution.py
+++ b/solution.py
@@ -74,8 +74,9 @@
     log_sum_exp = jnp.transpose(log_sum_exp, (2, 0, 1)).reshape(row_count, QUERY_HEADS)
     value_partial_sum, log_sum_exp = (value_partial_sum, log_sum_exp)
     value_partial_sum, log_sum_exp = (value_partial_sum, log_sum_exp)
-    received = lax.all_to_all(
-        value_partial_sum[None], "seq", split_axis=2, concat_axis=0, tiled=True
+    mine_x = value_partial_sum[None]
+    received = jnp.concatenate(
+        lax.all_to_all(jnp.stack(jnp.split(mine_x, lax.axis_size("seq"), 2)), "seq", 0, 0), 0
     )
     totals = lax.all_to_all(log_sum_exp[None], "seq", split_axis=2, concat_axis=0, tiled=True)
     merged = merge_sources(received, totals)

time: 310 us -> 324 us (1.045)
  local copies, waits for them, and re-layouts: 25.9 us -> 44.4 us
  blocking collectives: 9.87 us -> 0 us
  starting transfers between devices: 4.47 us -> 9.56 us
    unnamed x2 -> x19, local copies, waits for them, and re-layouts: 0.01 us -> 17.2 us
    all_to_all x1 -> x0, blocking collectives: 9.87 us -> none  [body(): lax.all_to_all(log_sum_exp[None], 'seq', split_axis=2, concat_axis=0, til...]
    all_to_all x1 -> x2, starting transfers between devices: 4.42 us -> 9.52 us  [the longest x1 6.02 us: body(): lax.all_to_all(jnp.stack(jnp.split(mine_x, lax.axis_size('seq'), 2)), 'se...]
    all_to_all x1 -> x2, waiting for transfers between devices: 40.8 us -> 40.9 us  [the longest x1 40.9 us: body(): lax.all_to_all(jnp.stack(jnp.split(mine_x, lax.axis_size('seq'), 2)), 'se...]
  transfers between devices with their start and end apart: 3 -> 4, of which waited for: 3 -> 3; matrix products, arithmetic and copies ran while one was open for 0% -> 6% of each run, Pallas kernels for 0% -> 0%
where the time goes in v1:
time: 324 us; the launch traced here: 321 us
  waiting for transfers between devices  173 us (53%)
  matrix products  49.7 us (15%)
  local copies, waits for them, and re-layouts  44.4 us (14%)
  loops' own time  20.5 us (6%)
  between operations  14.9 us (5%)
  starting transfers between devices  9.56 us (3%)
  other arithmetic  9 us (3%)
    reduce_scatter x1, waiting for transfers between devices, body(): lax.psum_scatter(jnp.dot(flattened, out_weight, preferred_element_type=jn...  86.6 us
    all_gather x1, waiting for transfers between devices, body(): piece_rows = lax.all_gather(query_block, 'seq', axis=0, tiled=True)  45 us
    all_to_all x1, waiting for transfers between devices, body(): lax.all_to_all(jnp.stack(jnp.split(mine_x, lax.axis_size('seq'), 2)), 'se...  40.9 us
    dot_general x16, matrix products, head_partial(): jnp.einsum('grk,kd->grd', weights.astype(jnp.bfloat16), value_cols, prefe...  29.3 us
    another operation x1, loops' own time, body(): lax.map(single_head, jnp.arange(KEY_VALUE_HEADS, dtype=jnp.int32))  20.5 us
    unnamed x19, local copies, waits for them, and re-layouts  17.2 us
    dot_general x16, matrix products, head_partial(): jnp.einsum('rgd,kd->grk', grouped, key_cols, preferred_element_type=jnp.f...  17.1 us
    dynamic_slice x32, local copies, waits for them, and re-layouts, single_head(): lax.dynamic_slice_in_dim(piece_rows, key_value_head * (group_width * HEAD...  16.3 us
  transfers between devices with their start and end apart: 4, of which 3 were waited for; matrix products, arithmetic and copies ran while one was open for 6% of the time, Pallas kernels for 0%

profile of v1, /device:TPU:0, one launch (start us, length us, event | category | flops | bytes accessed | tf_op | source)
XLA Modules:
  0.0 321.3 jit_solution(13580168559673217180)
XLA Ops:
  8.7 45.0 %all-gather.2.cloned.1.call-done = bf16[256,4096]{1,0:T(8,128)(2,1)} async-done(((bf16[16,4096]{1,0:T(8,128)(2,1)}), bf16[256,4096]{1,0:T(8,128)(2,1)}) %all-gather.2.cloned.1.call-update) | async-done | bytes 2097168 | tf_op jit(solution)/shard_map/all_gather | solution.py:51
  53.7 97.3 %while.13 = (s32[]{:T(128)}, bf16[16,2,256,128]{3,2,1,0:T(8,128)(2,1)}, f32[16,2,256]{2,1,0:T(2,128)S(1)}, s32[16]{0:T(128)S(1)}, bf16[256,2048]{1,0:T(8,128)(2,...) while((s32[]{:T(128)}, ...), condition=%wide.region_3.4_spmd.clone, body=%wide.region_0.3_spmd.clone.sunk | while | flops 68552712 | bytes 2775577 | solution.py:68
  58.0 1.8 fusion.56
  64.0 1.8 fusion.56
  70.1 1.8 fusion.56
  76.2 1.8 fusion.56
  82.3 1.8 fusion.56
  88.4 1.8 fusion.56
  94.4 1.8 fusion.56
  100.5 1.8 fusion.56
  106.6 1.8 fusion.56
  112.7 1.8 fusion.56
  118.8 1.8 fusion.56
  124.8 1.8 fusion.56
  130.9 1.8 fusion.56
  137.0 1.8 fusion.56
  143.1 1.8 fusion.56
  149.1 1.8 fusion.56
  151.6 3.5 %all-to-all-start = ((f32[1,256,32]{1,0,2:T(1,128)}), f32[1,256,32]{1,0,2:T(1,128)S(1)}, u32[]{:S(2)}, u32[]{:S(2)}) async-start(f32[1,256,32]{1,0,2:T(1,128)} %broadcast_in_dim_reshape.6), calls=%async_computation | async-start | bytes 65536 | tf_op jit(solution)/shard_map/all_to_all | solution.py:81
  173.0 6.0 %all-to-all-start.1 = ((bf16[16,1,256,2,128]{4,2,3,1,0:T(8,128)(2,1)}), bf16[16,1,256,2,128]{4,2,3,1,0:T(8,128)(2,1)}, u32[]{:S(2)}, u32[]{:S(2)}) async-start(bf16[16,1,256,2,128]{4,2,3,1,0:T(8,128)(2,1)} %fusion.23), calls=%async_computation.1 | async-start | bytes 4194304 | tf_op jit(solution)/shard_map/all_to_all | solution.py:79
  179.2 40.9 %all-to-all-done.1 = bf16[16,1,256,2,128]{4,2,3,1,0:T(8,128)(2,1)} async-done(((bf16[16,1,256,2,128]{4,2,3,1,0:T(8,128)(2,1)}), bf16[16,1,256,2,128]{4,2,3,1,0:T(8,128)(2,1)}, u32[]{:S(2)}, u32[]{:S(2)}) %all-to-all-start.1) | async-done | bytes 2097184 | tf_op jit(solution)/shard_map/all_to_all | solution.py:79
  220.1 2.5 fusion.22
  222.9 3.3 %fusion.42 = f32[256,5376]{1,0:T(8,128)} fusion(bf16[256,256]{0,1:T(8,128)(2,1)S(1)} %bitcast.146, bf16[256,5376]{1,0:T(8,128)(2,1)S(1)} %copy-done), kind=kOutput, calls=%fused_computation.71 | convolution fusion | flops 704643072 | bytes 8388608 | tf_op jit(solution)/shard_map/dot_general | solution.py:85
  226.2 86.6 %reduce-scatter.2.cloned.1.call-done = f32[16,5376]{1,0:T(8,128)} async-done(((f32[256,5376]{1,0:T(8,128)}), f32[16,5376]{1,0:T(8,128)}) %reduce-scatter.2.cloned.1.call-update) | async-done | bytes 344080 | tf_op jit(solution)/shard_map/reduce_scatter | solution.py:84
  (164 shorter events, 68.8 us)
Async XLA Ops:
  6.5 216.3 %copy-start = (bf16[256,5376]{1,0:T(8,128)(2,1)S(1)}, bf16[256,5376]{1,0:T(8,128)(2,1)}, u32[]{:S(2)}) copy-start(bf16[256,5376]{1,0:T(8,128)(2,1)} %param.13) | copy-start | bytes 8257540
  6.5 47.2 %all-gather.2.cloned.1.call-start = ((), (), s32[]{:S(2)}) async-start(), calls=%async_computation.3 | async-start | bytes 2228224 | tf_op jit(solution)/shard_map/all_gather | solution.py:51
  151.6 21.4 %all-to-all-start = ((f32[1,256,32]{1,0,2:T(1,128)}), f32[1,256,32]{1,0,2:T(1,128)S(1)}, u32[]{:S(2)}, u32[]{:S(2)}) async-start(f32[1,256,32]{1,0,2:T(1,128)} %broadcast_in_dim_reshape.6), calls=%async_computation | async-start | bytes 65536 | tf_op jit(solution)/shard_map/all_to_all | solution.py:81
  155.1 12.6 %copy-start.1 = (bf16[16,2,256,128]{3,2,1,0:T(8,128)(2,1)S(1)}, bf16[16,2,256,128]{3,2,1,0:T(8,128)(2,1)}, u32[]{:S(2)}) copy-start(bf16[16,2,256,128]{3,2,1,0:T(8,128)(2,1)} %get-tuple-element.49) | copy-start | bytes 6291460
  173.0 47.1 %all-to-all-start.1 = ((bf16[16,1,256,2,128]{4,2,3,1,0:T(8,128)(2,1)}), bf16[16,1,256,2,128]{4,2,3,1,0:T(8,128)(2,1)}, u32[]{:S(2)}, u32[]{:S(2)}) async-start(bf16[16,1,256,2,128]{4,2,3,1,0:T(8,128)(2,1)} %fusion.23), calls=%async_computation.1 | async-start | bytes 4194304 | tf_op jit(solution)/shard_map/all_to_all | solution.py:79
  179.1 133.8 %reduce-scatter.2.cloned.1.call-start = ((), (), s32[]{:S(2)}) async-start(), calls=%async_computation.4 | async-start | bytes 5849088 | tf_op jit(solution)/shard_map/reduce_scatter | solution.py:84
Sparse Core Ops, SparseCore 0:
  9.5 44.1 all-gather.1
  226.3 86.4 reduce-scatter.1
